TPU v7x, 128 devices: a whole 4x4x4 slice. The times are simulated.
128 devices in a mesh: dp: 64 (over y, x, z_lo, core), mp: 2 (over z_hi).
Axes of the slice: x: 4, y: 4, z: 4 (z_hi: 2, z_lo: 2; z = z_hi * 2 + z_lo), core: 2. Of those that a mesh axis runs over, the one named last changes fastest.
Arguments:
- clean_latent: float32 [64, 4096], P('dp'), may hold values from -6 to 6
- noise_draw: float32 [64, 4096], P('dp'), may hold values from -6 to 6
- timestep: int32 [64], P('dp'), may hold values from 1 to 8
- bucket: int32 [64], P('dp'), may hold values from 0 to 7
- bucket_weights: float32 [8], replicated, may hold values from 0.25 to 4
- teacher_embed: float32 [16, 2048], replicated, may hold values from -1.5 to 1.5
- teacher_final: float32 [16, 2048], replicated, may hold values from -0.125 to 0.125
- teacher_mod: float32 [16, 3, 2048], replicated, may hold values from -3 to 3
- teacher_qkv: bfloat16 [2048, 3, 1024], P(None, None, 'mp'), may hold values from -1 to 1
- teacher_out: bfloat16 [2048, 1024], P(None, 'mp'), may hold values from -0.1875 to 0.1875
- student_embed: float32 [16, 2048], replicated, may hold values from -1.5 to 1.5
- student_final: float32 [16, 2048], replicated, may hold values from -0.125 to 0.125
- student_mod: float32 [8, 3, 2048], replicated, may hold values from -3 to 3
- student_qkv: bfloat16 [2048, 3, 1024], P('dp', None, 'mp'), may hold values from -1 to 1
- student_out: bfloat16 [2048, 1024], P('dp', 'mp'), may hold values from -0.1875 to 0.1875
- moment_qkv: float32 [2048, 3, 1024], P('dp', None, 'mp'), may hold values from -2 to 2
- second_qkv: float32 [2048, 3, 1024], P('dp', None, 'mp'), may hold values from 0.05 to 0.5
- moment_out: float32 [2048, 1024], P('dp', 'mp'), may hold values from -2 to 2
- second_out: float32 [2048, 1024], P('dp', 'mp'), may hold values from 0.05 to 0.5
Outputs:
- new_moment_qkv: float32 [2048, 3, 1024], P('dp', None, 'mp')
- new_second_qkv: float32 [2048, 3, 1024], P('dp', None, 'mp')
- update_qkv: float32 [2048, 3, 1024], P('dp', None, 'mp')
- new_moment_out: float32 [2048, 1024], P('dp', 'mp')
- new_second_out: float32 [2048, 1024], P('dp', 'mp')
- update_out: float32 [2048, 1024], P('dp', 'mp')
- loss: float32 [], replicated
All inputs are finite; a program needn't handle non-finite values.
Results may differ from a plain program's by a relative error of at most 0.00035.
Values may be sent and summed in bfloat16 or wider, within the bound.
A program may use at most 128 MiB of HBM per device.

v0:
```python
import math
import jax
import jax.numpy as jnp
from jax import lax
from jax.sharding import Mesh
from jax.sharding import PartitionSpec as P

D = 2048
HS = 64
INNER = 1024
PATCH_CH = 16
SEQ = 256
LATENT = 4096
K = 8
TGRID = 16
NBUCKET = 8
DP = ("dp_0", "dp_1", "dp_2", "dp_3")
DP_MP = ("dp_0", "dp_1", "dp_2", "dp_3", "mp")
LN_EPS = 0.01
BETA_ONE = 0.9
BETA_TWO = 0.99
ADAM_EPS = 1e-08


def in_blocks(shard, dim, devices):
    before, after = (shard.shape[:dim], shard.shape[dim + 1 :])
    return jnp.moveaxis(shard.reshape(*before, devices, -1, *after), dim, 0)


def summed_on_arrival(shard, axis, dim):
    devices = lax.axis_size(axis)
    parts = lax.all_to_all(in_blocks(shard, dim, devices), axis, 0, 0, tiled=True)
    return jnp.sum(parts, axis=0)


def side_by_side(arrays, axis, dim, along):
    widths = [math.prod(a.shape[along:]) for a in arrays]
    both = jnp.concatenate(
        [a.reshape(*a.shape[:along], w) for a, w in zip(arrays, widths)], axis=along
    )
    whole = lax.all_gather(both, axis, axis=dim, tiled=True)
    parts = jnp.split(whole, [sum(widths[:k]) for k in range(1, len(widths))], axis=along)
    return tuple((b.reshape(*whole.shape[:along], *a.shape[along:]) for a, b in zip(arrays, parts)))


def in_order(parts, dim):
    parts = jnp.moveaxis(parts, 0, dim)
    dims = parts.shape
    return parts.reshape(*dims[:dim], dims[dim] * dims[dim + 1], *dims[dim + 2 :])


def sent_to_all(shard, axis):
    copies = jnp.broadcast_to(shard, (lax.axis_size(axis), *shard.shape))
    return lax.all_to_all(copies, axis, split_axis=0, concat_axis=0, tiled=True)


def gathered_copies(shard, axis, dim):
    return in_order(sent_to_all(shard, axis), dim)


def by_axis(shard, axes):
    for axis in axes:
        shard = lax.psum(shard, axis)
    return shard


def summed_rows_2(shard, chips, core, dim):
    sizes = (lax.axis_size(chips), lax.axis_size(core))
    parts = in_blocks(shard, dim, sizes[0] * sizes[1])
    inside = parts.shape[1:]
    parts = parts.reshape(*sizes, *inside).swapaxes(0, 1).reshape(-1, *inside)
    parts = lax.psum_scatter(parts, core, scatter_dimension=0, tiled=True)
    return lax.psum_scatter(parts, chips, scatter_dimension=0, tiled=True)[0]


def plan():
    grid = jnp.arange(TGRID + 1, dtype=jnp.float32)
    lamb = 6.0 - 12.0 * grid / TGRID
    return (jnp.sqrt(jax.nn.sigmoid(lamb)), jnp.sqrt(jax.nn.sigmoid(-lamb)))


def positions():
    index = jnp.arange(SEQ, dtype=jnp.float32)[:, None]
    half = D // 2
    freqs = jnp.exp(-math.log(10000.0) * jnp.arange(half, dtype=jnp.float32) / half)
    angles = index * freqs[None, :]
    return jnp.concatenate([jnp.sin(angles), jnp.cos(angles)], axis=1)


def normalize(values):
    center = values - jnp.mean(values, axis=-1, keepdims=True)
    inverse = lax.rsqrt(jnp.mean(center * center, axis=-1, keepdims=True) + LN_EPS)
    return (center * inverse, inverse)


def norm_back(upstream, normed, inverse):
    first_mean = jnp.mean(upstream, axis=-1, keepdims=True)
    second_mean = jnp.mean(upstream * normed, axis=-1, keepdims=True)
    return (upstream - first_mean - normed * second_mean) * inverse


def one_hot_rows(index, width):
    return (index[:, None] == jnp.arange(width, dtype=jnp.int32)[None, :]).astype(jnp.float32)


def per_device(
    clean_latent,
    noise_draw,
    timestep,
    bucket,
    bucket_weights,
    teacher_embed,
    teacher_final,
    teacher_mod,
    teacher_qkv,
    teacher_out,
    student_embed,
    student_final,
    student_mod,
    student_qkv,
    student_out,
    moment_qkv,
    second_qkv,
    moment_out,
    second_out,
):
    samples = clean_latent.shape[0]
    rows_all = samples * SEQ
    local_inner = teacher_out.shape[1]
    local_heads = local_inner // HS
    count = rows_all // lax.axis_size("mp")
    start = lax.axis_index("mp") * count

    def take(values):
        return lax.dynamic_slice_in_dim(values, start, count, 0)

    alphas, sigmas = plan()
    table = jnp.stack([alphas, sigmas], axis=1)

    def coefficients(tau):
        picked = jnp.dot(one_hot_rows(tau, TGRID + 1), table, precision=lax.Precision.HIGHEST)
        picked = jnp.repeat(picked, SEQ, axis=0)
        return (picked[:, 0:1], picked[:, 1:2])

    def modulation(mod_table, index, length):
        picked = jnp.dot(
            one_hot_rows(index, length),
            mod_table.reshape(length, 3 * D),
            precision=lax.Precision.HIGHEST,
        )
        return picked.reshape(samples, 3, D)

    def gate_rows(modrows):
        return take(jnp.repeat(modrows[:, 2], SEQ, axis=0))

    placed = positions()

    def front(latent, modrows, embed, w_qkv, w_out):
        hidden = (
            jnp.dot(latent, embed, precision=lax.Precision.HIGHEST).reshape(samples, SEQ, D)
            + placed[None]
        )
        normed, unused = normalize(hidden)
        shaped = (
            (normed * (1.0 + modrows[:, None, 1]) + modrows[:, None, 0])
            .astype(jnp.bfloat16)
            .reshape(rows_all, D)
        )
        hidden = hidden.reshape(rows_all, D)
        packed = jnp.dot(
            shaped, w_qkv.reshape(D, 3 * local_inner), preferred_element_type=jnp.float32
        )
        packed = packed.astype(jnp.bfloat16).reshape(samples, SEQ, 3, local_heads, HS)
        queries = packed[:, :, 0]
        keys_all = packed[:, :, 1]
        values = packed[:, :, 2]
        scores = jnp.einsum(
            "sqhd,skhd->shqk", queries, keys_all, preferred_element_type=jnp.float32
        ) / math.sqrt(HS)
        highest = jnp.max(scores, axis=-1, keepdims=True)
        expos = jnp.exp(scores - highest)
        weights = expos / jnp.sum(expos, axis=-1, keepdims=True)
        rounded = weights.astype(jnp.bfloat16)
        attended = jnp.einsum(
            "shqk,skhd->sqhd", rounded, values, preferred_element_type=jnp.float32
        )
        attended = attended.astype(jnp.bfloat16).reshape(rows_all, local_inner)
        projected = lax.dot_general(
            attended, w_out, (((1,), (1,)), ((), ())), preferred_element_type=jnp.float32
        )
        return (hidden, shaped, queries, keys_all, values, weights, rounded, attended, projected)

    def reduce_heads(projected):
        return summed_on_arrival(projected, "mp", 0)

    def tail(hidden, modrows, projected, final):
        mixed = take(hidden) + gate_rows(modrows) * reduce_heads(projected)
        normed, inverse = normalize(mixed)
        predicted = lax.dot_general(
            normed, final, (((1,), (1,)), ((), ())), precision=lax.Precision.HIGHEST
        )
        return (predicted, normed, inverse)

    def teacher_eps(latent, modrows):
        parts = front(latent, modrows, teacher_embed, teacher_qkv, teacher_out)
        return tail(parts[0], modrows, parts[8], teacher_final)[0]

    whole_qkv, whole_out = side_by_side((student_qkv, student_out), DP, 0, 1)
    first = 2 * timestep
    middle = first - 1
    last = first - 2
    a_first, s_first = coefficients(first)
    a_middle, s_middle = coefficients(middle)
    a_last, s_last = coefficients(last)
    clean_rows = clean_latent.reshape(rows_all, PATCH_CH)
    noise_rows = noise_draw.reshape(rows_all, PATCH_CH)
    latent0 = a_first * clean_rows + s_first * noise_rows
    mine0 = take(latent0)
    af_mine, sf_mine = (take(a_first), take(s_first))
    am_mine, sm_mine = (take(a_middle), take(s_middle))
    al_mine, sl_mine = (take(a_last), take(s_last))
    eps_zero = teacher_eps(latent0, modulation(teacher_mod, first - 1, TGRID))
    next_mine = am_mine * (mine0 - sf_mine * eps_zero) / af_mine + sm_mine * eps_zero
    latent1 = gathered_copies(next_mine, "mp", 0)
    eps_one = teacher_eps(latent1, modulation(teacher_mod, middle - 1, TGRID))
    latent2 = al_mine * (take(latent1) - sm_mine * eps_one) / am_mine + sl_mine * eps_one
    target = (mine0 - af_mine / al_mine * latent2) / (sf_mine - af_mine * sl_mine / al_mine)
    student_rows_mod = modulation(student_mod, timestep - 1, K)
    hidden, shaped, queries, keys_all, values, weights, rounded, attended, projected = front(
        latent0, student_rows_mod, student_embed, whole_qkv, whole_out
    )
    predicted, normed, inverse = tail(hidden, student_rows_mod, projected, student_final)
    sample_weight = jnp.dot(
        one_hot_rows(bucket, NBUCKET), bucket_weights, precision=lax.Precision.HIGHEST
    )
    row_weight = take(jnp.repeat(sample_weight, SEQ, axis=0)[:, None])
    error = predicted - target
    loss_part = jnp.sum(row_weight * error * error)
    d_pred = 2.0 * row_weight * error
    d_normed = jnp.dot(d_pred, student_final, precision=lax.Precision.HIGHEST)
    d_mixed = norm_back(d_normed, normed, inverse)
    d_proj_mine = (gate_rows(student_rows_mod) * d_mixed).astype(jnp.bfloat16)
    d_proj = gathered_copies(d_proj_mine, "mp", 0)
    loss_sum = by_axis(loss_part, DP_MP)
    d_attn = jnp.dot(d_proj, whole_out, preferred_element_type=jnp.float32).astype(jnp.bfloat16)
    d_attn = d_attn.reshape(samples, SEQ, local_heads, HS)
    d_prob = jnp.einsum("sqhd,skhd->shqk", d_attn, values, preferred_element_type=jnp.float32)
    d_score = (
        weights * (d_prob - jnp.sum(weights * d_prob, axis=-1, keepdims=True)) / math.sqrt(HS)
    ).astype(jnp.bfloat16)
    d_query = jnp.einsum(
        "shqk,skhd->sqhd", d_score, keys_all, preferred_element_type=jnp.float32
    ).astype(jnp.bfloat16)
    d_key = jnp.einsum(
        "shqk,sqhd->skhd", d_score, queries, preferred_element_type=jnp.float32
    ).astype(jnp.bfloat16)
    d_value = jnp.einsum(
        "shqk,sqhd->skhd", rounded, d_attn, preferred_element_type=jnp.float32
    ).astype(jnp.bfloat16)
    d_pack = jnp.stack([d_query, d_key, d_value], axis=2).reshape(rows_all, 3 * local_inner)
    own_rows = D // lax.axis_size(DP)
    piece = shaped
    grad_qkv = lax.psum_scatter(
        lax.dot_general(
            piece, d_pack, (((0,), (0,)), ((), ())), preferred_element_type=jnp.float32
        ),
        DP,
        scatter_dimension=0,
        tiled=True,
    ).reshape(own_rows, 3, local_inner)
    piece = d_proj
    grad_out = summed_rows_2(
        lax.dot_general(
            piece, attended, (((0,), (0,)), ((), ())), preferred_element_type=jnp.float32
        ),
        ("dp_0", "dp_1", "dp_2"),
        "dp_3",
        0,
    )
    squares = jnp.sum(grad_qkv * grad_qkv) + jnp.sum(grad_out * grad_out)
    squares = by_axis(squares, DP_MP)
    rms_value = jnp.sqrt(squares / (4 * D * INNER))
    factor = 1.0 / jnp.maximum(rms_value, 1.0)

    def adam(moment, second, grad):
        normed_grad = grad * factor
        new_moment = BETA_ONE * moment + (1.0 - BETA_ONE) * normed_grad
        new_second = BETA_TWO * second + (1.0 - BETA_TWO) * normed_grad * normed_grad
        return (new_moment, new_second, new_moment / (jnp.sqrt(new_second) + ADAM_EPS))

    mq, vq, uq = adam(moment_qkv, second_qkv, grad_qkv)
    mo, vo, uo = adam(moment_out, second_out, grad_out)
    loss = loss_sum / (samples * lax.axis_size(DP) * LATENT)
    return (mq, vq, uq, mo, vo, uo, loss)


def solution(mesh):
    torus = Mesh(
        mesh.devices.reshape(4, 4, 2, 2, mesh.shape["mp"]), ("dp_0", "dp_1", "dp_2", "dp_3", "mp")
    )
    in_specs = (
        P(DP, None),
        P(DP, None),
        P(DP),
        P(DP),
        P(),
        P(),
        P(),
        P(),
        P(None, None, "mp"),
        P(None, "mp"),
        P(),
        P(),
        P(),
        P(DP, None, "mp"),
        P(DP, "mp"),
        P(DP, None, "mp"),
        P(DP, None, "mp"),
        P(DP, "mp"),
        P(DP, "mp"),
    )
    out_specs = (
        P(DP, None, "mp"),
        P(DP, None, "mp"),
        P(DP, None, "mp"),
        P(DP, "mp"),
        P(DP, "mp"),
        P(DP, "mp"),
        P(),
    )
    return jax.shard_map(
        per_device, mesh=torus, in_specs=in_specs, out_specs=out_specs, check_vma=False
    )
```

profile of v0, /device:TPU:10, one launch (start us, length us, event | category | flops | bytes accessed | tf_op | source)
XLA Modules:
  0.0 784.5 jit_solution(3109990404546934198)
XLA Ops:
  8.3 1.4 pad_maximum_fusion.2
  11.1 2.1 add_reduce_fusion
  13.3 8.9 %copy.110 = bf16[2048,3,512]{0,2,1:T(8,128)(2,1)} copy(bf16[2048,3,512]{2,0,1:T(8,128)(2,1)} %param.27) | data formatting | bytes 12582912 | tf_op args[8]
  22.2 3.7 fusion.66
  25.9 2.0 fusion.162
  29.9 2.8 convolution_convert_fusion.1
  32.7 2.3 copy.111
  35.0 1.9 fusion.163
  36.8 2.9 fusion.45
  40.8 2.1 fusion.11
  42.9 5.8 all-to-all-start.1
  48.9 3.2 fusion.160
  52.1 1.3 copy-done.2
  57.0 18.7 %all-to-all-done.1 = f32[2,128,2048]{2,1,0:T(8,128)} async-done(((f32[2,128,2048]{2,1,0:T(8,128)}), f32[2,128,2048]{2,1,0:T(8,128)}, u32[]{:S(2)}, u32[]{:S(2)}) %all-to-all-start.1) | async-done | bytes 2097184 | tf_op jit(solution)/shard_map/all_to_all | solution.py:32
  75.7 2.8 reduce_sum.225
  78.6 1.8 fusion.152
  80.7 3.6 multiply_add_fusion.3
  84.9 3.2 all-to-all-start.2
  93.5 3.3 fusion.164
  98.1 4.8 convolution_convert_fusion
  102.8 1.2 copy.115
  104.1 1.9 fusion.165
  107.2 2.1 fusion.9
  109.2 5.1 all-to-all-start.3
  115.6 24.7 %all-to-all-done.3 = f32[2,128,2048]{2,1,0:T(8,128)} async-done(((f32[2,128,2048]{2,1,0:T(8,128)}), f32[2,128,2048]{2,1,0:T(8,128)}, u32[]{:S(2)}, u32[]{:S(2)}) %all-to-all-start.3) | async-done | bytes 2097184 | tf_op jit(solution)/shard_map/all_to_all | solution.py:32
  140.3 2.8 reduce_sum.231
  143.1 5.6 fusion.6
  148.7 1.4 copy.105
  150.1 2.2 fusion.161
  152.3 1.9 convolution_convert_fusion.5
  154.3 3.7 fusion.13
  158.0 4.8 all-to-all-start
  162.9 1.8 fusion.151
  164.9 1.6 fusion.48
  166.6 21.4 %all-to-all-done = f32[2,128,2048]{2,1,0:T(8,128)} async-done(((f32[2,128,2048]{2,1,0:T(8,128)}), f32[2,128,2048]{2,1,0:T(8,128)}, u32[]{:S(2)}, u32[]{:S(2)}) %all-to-all-start) | async-done | bytes 2097184 | tf_op jit(solution)/shard_map/all_to_all | solution.py:32
  188.0 2.9 reduce_sum.219
  190.9 1.5 fusion.153
  192.7 4.7 fusion.104
  197.4 1.3 fusion.146
  198.7 1.5 multiply_convert_fusion.1
  200.2 2.1 copy.118
  202.3 1.2 broadcast_in_dim.5
  203.5 16.2 %all_to_all.25 = bf16[2,128,2048]{1,2,0:T(8,128)(2,1)} all-to-all(bf16[2,128,2048]{1,2,0:T(8,128)(2,1)S(1)} %broadcast_in_dim.5), channel_id=1, replica_groups=mesh['dp_0'=4,'dp_1'=4,'dp_2'=2,'dp_3'=2,'mp'=2] {'mp'}, dimensions={0} | all-to-all | bytes 2097152 | tf_op jit(solution)/shard_map/all_to_all | solution.py:54
  219.7 1.5 copy.119
  221.2 1.4 copy.124
  222.6 2.0 convolution_bitcast_fusion
  224.5 2.5 copy.126
  227.1 29.4 %reduce-scatter.6.cloned.1.call-done = f32[32,32,512]{2,1,0:T(8,128)} async-done(((f32[64,32,512]{2,1,0:T(8,128)}), f32[32,32,512]{2,1,0:T(8,128)}) %reduce-scatter.6.cloned.1.call-update) | async-done | bytes 2097168 | tf_op jit(solution)/shard_map/reduce_scatter | solution.py:72
  256.8 2.3 fusion.36
  259.2 2.9 fusion.91
  262.1 4.5 fusion.42
  266.6 5.2 fusion.39
  271.8 2.1 fusion.47
  274.0 6.6 fusion.145
  280.6 126.1 %reduce-scatter.8.cloned.1.call-done = f32[1,32,512]{2,1,0:T(8,128)} async-done(((f32[32,32,512]{2,1,0:T(8,128)}), f32[1,32,512]{2,1,0:T(8,128)}) %reduce-scatter.8.cloned.1.call-update) | async-done | bytes 65552 | tf_op jit(solution)/shard_map/reduce_scatter | solution.py:73
  406.8 1.5 multiply_reduce_fusion.12
  408.3 276.5 %reduce-scatter.4.cloned.1.call-done = f32[32,1536]{1,0:T(8,128)} async-done(((f32[2048,1536]{1,0:T(8,128)}), f32[32,1536]{1,0:T(8,128)}) %reduce-scatter.4.cloned.1.call-update) | async-done | bytes 196624 | tf_op jit(solution)/shard_map/reduce_scatter | solution.py:263
  684.8 1.7 multiply_reduce_fusion.11
  687.9 47.4 %all-reduce.1 = (f32[]{:T(128)}, f32[]{:T(128)}) all-reduce(f32[]{:T(128)S(6)} %add.251, f32[]{:T(128)} %get-tuple-element.75), channel_id=1, replica_groups=mesh['dp_0'=4,'dp_1'=4,'dp_2'=2,'dp_3'=2,'mp'=2] {'dp_0'}, use_global_device_ids=true, to_apply=%region_29.0 | all-reduce | flops 2 | bytes 16 | tf_op jit(solution)/shard_map/psum | solution.py:63
  735.2 18.8 %all-reduce = (f32[]{:T(128)}, f32[]{:T(128)}) all-reduce(f32[]{:T(128)} %get-tuple-element.32, f32[]{:T(128)} %get-tuple-element.33), channel_id=1, replica_groups=mesh['dp_0'=4,'dp_1'=4,'dp_2'=2,'dp_3'=2,'mp'=2] {'dp_1'}, use_global_device_ids=true, to_apply=%region_30.0 | all-reduce | flops 2 | bytes 16 | tf_op jit(solution)/shard_map/psum | solution.py:63
  754.1 5.5 all-reduce.4
  759.6 3.1 all-reduce.3
  762.7 7.0 all-reduce.2
  771.6 1.4 add_divide_fusion
  (137 shorter events, 18.7 us)
Async XLA Ops:
  7.2 33.6 %copy-start = (bf16[2048,512]{1,0:T(8,128)(2,1)S(1)}, bf16[2048,512]{1,0:T(8,128)(2,1)}, u32[]{:S(2)}) copy-start(bf16[2048,512]{1,0:T(8,128)(2,1)} %param.28) | copy-start | bytes 6291460
  7.2 135.9 %all-gather.2.cloned.1.call-start = ((), (), s32[]{:S(2)}) async-start(), calls=%async_computation.8 | async-start | bytes 8519680 | tf_op jit(solution)/shard_map/all_gather | solution.py:41
  22.2 3.7 copy-start.13
  25.9 2.0 copy-start.4
  25.9 2.4 copy-start.8
  25.9 4.0 copy-start.7
  27.9 1.4 copy-start.5
  42.9 6.0 copy-start.21
  42.9 32.9 %all-to-all-start.1 = ((f32[2,128,2048]{2,1,0:T(8,128)}), f32[2,128,2048]{2,1,0:T(8,128)}, u32[]{:S(2)}, u32[]{:S(2)}) async-start(f32[2,128,2048]{2,1,0:T(8,128)} %fusion.11), calls=%async_computation.1 | async-start | bytes 4194304 | tf_op jit(solution)/shard_map/all_to_all | solution.py:32
  52.1 1.3 copy-start.2
  52.1 1.7 copy-start.19
  52.1 1.9 copy-start.9
  52.1 91.0 %copy-start.29 = (f32[256]{0:T(256)}, f32[256]{0:T(256)S(1)}, u32[]{:S(2)}) copy-start(f32[256]{0:T(256)S(1)} %broadcast_multiply_fusion.3) | copy-start | bytes 3076
  53.8 89.3 %copy-start.31 = (f32[256]{0:T(256)}, f32[256]{0:T(256)S(1)}, u32[]{:S(2)}) copy-start(f32[256]{0:T(256)S(1)} %add_rsqrt_fusion.2) | copy-start | bytes 3076
  55.0 25.7 %copy-start.22 = (f32[128,16]{0,1:T(8,128)}, f32[128,16]{0,1:T(8,128)S(1)}, u32[]{:S(2)}) copy-start(f32[128,16]{0,1:T(8,128)S(1)} %copy.148) | copy-start | bytes 24580
  78.6 2.1 copy-start.16
  78.6 9.6 %copy-start.33 = (f32[8]{0:T(128)S(1)}, f32[8]{0:T(128)}, u32[]{:S(2)}) copy-start(f32[8]{0:T(128)} %param.23) | copy-start | bytes 100
  78.6 14.9 %copy-start.14 = (f32[16,2048]{1,0:T(8,128)S(1)}, f32[16,2048]{1,0:T(8,128)}, u32[]{:S(2)}) copy-start(f32[16,2048]{1,0:T(8,128)} %param.24) | copy-start | bytes 393220
  84.9 8.6 %all-to-all-start.2 = ((f32[2,128,16]{1,2,0:T(8,128)}), f32[2,128,16]{1,2,0:T(8,128)S(1)}, u32[]{:S(2)}, u32[]{:S(2)}) async-start(f32[2,128,16]{1,2,0:T(8,128)} %broadcast_in_dim.4), calls=%async_computation.2 | async-start | bytes 32768 | tf_op jit(solution)/shard_map/all_to_all | solution.py:54
  96.7 1.4 copy-start.6
  104.1 1.9 copy-start.12
  109.2 31.0 %all-to-all-start.3 = ((f32[2,128,2048]{2,1,0:T(8,128)}), f32[2,128,2048]{2,1,0:T(8,128)}, u32[]{:S(2)}, u32[]{:S(2)}) async-start(f32[2,128,2048]{2,1,0:T(8,128)} %fusion.9), calls=%async_computation.3 | async-start | bytes 4194304 | tf_op jit(solution)/shard_map/all_to_all | solution.py:32
  114.3 28.8 %copy-start.3 = (f32[256,2048]{1,0:T(8,128)S(1)}, f32[256,2048]{1,0:T(8,128)}, u32[]{:S(2)}) copy-start(f32[256,2048]{1,0:T(8,128)} %copy-done.2) | copy-start | bytes 6291460
  150.1 4.1 copy-start.10
  152.3 1.9 copy-start.34
  158.0 29.9 %all-to-all-start = ((f32[2,128,2048]{2,1,0:T(8,128)}), f32[2,128,2048]{2,1,0:T(8,128)}, u32[]{:S(2)}, u32[]{:S(2)}) async-start(f32[2,128,2048]{2,1,0:T(8,128)} %fusion.13), calls=%async_computation | async-start | bytes 4194304 | tf_op jit(solution)/shard_map/all_to_all | solution.py:32
  162.9 93.6 %reduce-scatter.6.cloned.1.call-start = ((), (), s32[]{:S(2)}) async-start(), calls=%async_computation.10 | async-start | bytes 6291456 | tf_op jit(solution)/shard_map/reduce_scatter | solution.py:72
  166.6 24.3 %copy-start.24 = (f32[1,1,2048]{2,0,1:T(1,128)S(1)}, f32[1,1,2048]{2,0,1:T(1,128)}, u32[]{:S(2)}) copy-start(f32[1,1,2048]{2,0,1:T(1,128)} %get-tuple-element.56) | copy-start | bytes 24580
  190.9 1.8 copy-start.15
  190.9 1.8 copy-start.23
  190.9 1.8 copy-start.27
  190.9 1.8 copy-start.28
  227.0 179.7 %reduce-scatter.8.cloned.1.call-start = ((), (), s32[]{:S(2)}) async-start(), calls=%async_computation.11 | async-start | bytes 2162688 | tf_op jit(solution)/shard_map/reduce_scatter | solution.py:73
  256.5 428.3 %reduce-scatter.4.cloned.1.call-start = ((), (), s32[]{:S(2)}) async-start(), calls=%async_computation.9 | async-start | bytes 12779520 | tf_op jit(solution)/shard_map/reduce_scatter | solution.py:263
  259.1 3.0 copy-start.11
  259.1 3.0 copy-start.35
  271.8 2.1 copy-start.18
  271.8 2.2 copy-start.30
  271.8 2.2 copy-start.32
  280.6 491.0 %copy-start.20 = (f32[32,3,512]{2,0,1:T(8,128)S(1)}, f32[32,3,512]{2,0,1:T(8,128)}, u32[]{:S(2)}) copy-start(f32[32,3,512]{2,0,1:T(8,128)} %param.35) | copy-start | bytes 589828
  280.6 495.3 %copy-start.25 = (f32[32,512]{1,0:T(8,128)S(1)}, f32[32,512]{1,0:T(8,128)}, u32[]{:S(2)}) copy-start(f32[32,512]{1,0:T(8,128)} %param.37) | copy-start | bytes 196612
  280.6 495.3 %copy-start.26 = (f32[32,512]{1,0:T(8,128)S(1)}, f32[32,512]{1,0:T(8,128)}, u32[]{:S(2)}) copy-start(f32[32,512]{1,0:T(8,128)} %param.36) | copy-start | bytes 196612
  406.8 369.1 %copy-start.17 = (f32[1,32,512]{2,1,0:T(8,128)S(1)}, f32[1,32,512]{2,1,0:T(8,128)}, u32[]{:S(2)}) copy-start(f32[1,32,512]{2,1,0:T(8,128)} %reduce-scatter.8.cloned.1.call-done) | copy-start | bytes 196612
  684.8 91.8 %copy-start.1 = (bf16[2048,512]{1,0:T(8,128)(2,1)S(1)}, bf16[2048,512]{1,0:T(8,128)(2,1)}, u32[]{:S(2)}) copy-start(bf16[2048,512]{1,0:T(8,128)(2,1)} %param.28) | copy-start | bytes 6291460
Sparse Core Ops, SparseCore 0:
  10.3 113.7 all-gather.1
  227.1 29.3 reduce-scatter.5
  258.9 147.8 reduce-scatter.7
  409.0 275.7 reduce-scatter.3
where the time goes:
time: 794 us; the launch traced here: 784 us
  waiting for transfers between devices  497 us (63%)
  blocking collectives  98.1 us (12%)
  matrix products  79.1 us (10%)
  local copies, waits for them, and re-layouts  35.3 us (4%)
  other arithmetic  31.2 us (4%)
  between operations  24.3 us (3%)
  starting transfers between devices  19.3 us (2%)
    reduce_scatter x1, waiting for transfers between devices, per_device(): lax.psum_scatter(lax.dot_general(piece, d_pack, (((0,), (0,)), ((), ())),...  277 us
    reduce_scatter x1, waiting for transfers between devices, summed_rows_2(): return lax.psum_scatter(parts, chips, scatter_dimension=0, tiled=True)[0]  126 us
    psum x5, blocking collectives, by_axis(): shard = lax.psum(shard, axis)  81.9 us
    all_to_all x3, waiting for transfers between devices, summed_on_arrival(): lax.all_to_all(in_blocks(shard, dim, devices), axis, 0, 0, tiled=True)  64.8 us
    reduce_scatter x1, waiting for transfers between devices, summed_rows_2(): parts = lax.psum_scatter(parts, core, scatter_dimension=0, tiled=True)  29.4 us
    all_to_all x1, blocking collectives, sent_to_all(): return lax.all_to_all(copies, axis, split_axis=0, concat_axis=0, tiled=True)  16.2 us
  transfers between devices with their start and end apart: 8, of which 7 were waited for; matrix products, arithmetic and copies ran while one was open for 12% of the time, Pallas kernels for 0%

commit v1 on v0

--- a/solution.py
+++ b/solution.py
@@ -60,7 +60,7 @@
 
 def by_axis(shard, axes):
     for axis in axes:
-        shard = lax.psum(shard, axis)
+        shard = jnp.sum(lax.all_gather(shard, axis), axis=0)
     return shard
 
 

time: 794 us -> 810 us (1.020)
  local copies, waits for them, and re-layouts: 35.3 us -> 51.6 us
    psum x5 -> x0, blocking collectives: 81.9 us -> none  [by_axis(): shard = lax.psum(shard, axis)]
    unnamed x0 -> x5, blocking collectives: none -> 79.8 us
    unnamed x77 -> x114, local copies, waits for them, and re-layouts: 14.8 us -> 32.1 us
where the time goes in v1:
time: 810 us; the launch traced here: 800 us
  waiting for transfers between devices  497 us (61%)
  blocking collectives  96.1 us (12%)
  matrix products  80.3 us (10%)
  local copies, waits for them, and re-layouts  51.6 us (6%)
  other arithmetic  31.5 us (4%)
  between operations  24.5 us (3%)
  starting transfers between devices  19.5 us (2%)
    reduce_scatter x1, waiting for transfers between devices, per_device(): lax.psum_scatter(lax.dot_general(piece, d_pack, (((0,), (0,)), ((), ())),...  278 us
    reduce_scatter x1, waiting for transfers between devices, summed_rows_2(): return lax.psum_scatter(parts, chips, scatter_dimension=0, tiled=True)[0]  123 us
    unnamed x5, blocking collectives  79.8 us
    all_to_all x3, waiting for transfers between devices, summed_on_arrival(): lax.all_to_all(in_blocks(shard, dim, devices), axis, 0, 0, tiled=True)  65.9 us
    unnamed x114, local copies, waits for them, and re-layouts  32.1 us
    reduce_scatter x1, waiting for transfers between devices, summed_rows_2(): parts = lax.psum_scatter(parts, core, scatter_dimension=0, tiled=True)  30 us
    all_to_all x1, blocking collectives, sent_to_all(): return lax.all_to_all(copies, axis, split_axis=0, concat_axis=0, tiled=True)  16.3 us
  transfers between devices with their start and end apart: 8, of which 7 were waited for; matrix products, arithmetic and copies ran while one was open for 12% of the time, Pallas kernels for 0%

profile of v1, /device:TPU:10, one launch (start us, length us, event | category | flops | bytes accessed | tf_op | source)
XLA Modules:
  0.0 800.4 jit_solution(6539303337243164906)
XLA Ops:
  8.3 1.4 pad_maximum_fusion.2
  11.2 2.1 add_reduce_fusion
  13.4 8.9 %copy.110 = bf16[2048,3,512]{0,2,1:T(8,128)(2,1)} copy(bf16[2048,3,512]{2,0,1:T(8,128)(2,1)} %param.27) | data formatting | bytes 12582912 | tf_op args[8]
  22.2 3.7 fusion.66
  26.0 2.0 fusion.162
  29.9 2.8 convolution_convert_fusion.1
  32.7 2.3 copy.111
  35.0 1.9 fusion.163
  36.9 2.9 fusion.45
  40.8 2.1 fusion.11
  42.9 5.8 all-to-all-start.1
  48.9 3.2 fusion.160
  57.1 18.7 %all-to-all-done.1 = f32[2,128,2048]{2,1,0:T(8,128)} async-done(((f32[2,128,2048]{2,1,0:T(8,128)}), f32[2,128,2048]{2,1,0:T(8,128)}, u32[]{:S(2)}, u32[]{:S(2)}) %all-to-all-start.1) | async-done | bytes 2097184 | tf_op jit(solution)/shard_map/all_to_all | solution.py:32
  75.8 2.8 reduce_sum.315
  78.6 1.8 fusion.152
  80.7 3.6 multiply_add_fusion.3
  84.9 3.2 all-to-all-start.2
  93.5 3.3 fusion.164
  98.1 4.8 convolution_convert_fusion
  104.1 1.9 fusion.165
  107.2 2.1 fusion.9
  109.2 5.1 all-to-all-start.3
  115.6 24.8 %all-to-all-done.3 = f32[2,128,2048]{2,1,0:T(8,128)} async-done(((f32[2,128,2048]{2,1,0:T(8,128)}), f32[2,128,2048]{2,1,0:T(8,128)}, u32[]{:S(2)}, u32[]{:S(2)}) %all-to-all-start.3) | async-done | bytes 2097184 | tf_op jit(solution)/shard_map/all_to_all | solution.py:32
  140.4 1.8 reduce_sum.321
  142.3 5.6 fusion.6
  147.8 2.3 copy.105
  150.1 3.2 fusion.161
  153.4 2.7 convolution_convert_fusion.5
  157.1 3.8 fusion.13
  160.9 4.9 all-to-all-start
  165.9 1.4 fusion.151
  168.6 22.4 %all-to-all-done = f32[2,128,2048]{2,1,0:T(8,128)} async-done(((f32[2,128,2048]{2,1,0:T(8,128)}), f32[2,128,2048]{2,1,0:T(8,128)}, u32[]{:S(2)}, u32[]{:S(2)}) %all-to-all-start) | async-done | bytes 2097184 | tf_op jit(solution)/shard_map/all_to_all | solution.py:32
  191.0 1.8 reduce_sum.309
  193.7 4.8 fusion.104
  200.7 16.3 %all_to_all.25 = bf16[2,128,2048]{1,2,0:T(8,128)(2,1)} all-to-all(bf16[2,128,2048]{1,2,0:T(8,128)(2,1)S(1)} %broadcast_in_dim.5), channel_id=1, replica_groups=mesh['dp_0'=4,'dp_1'=4,'dp_2'=2,'dp_3'=2,'mp'=2] {'mp'}, dimensions={0} | all-to-all | bytes 2097152 | tf_op jit(solution)/shard_map/all_to_all | solution.py:54
  217.0 1.5 copy.119
  218.5 1.4 copy.124
  219.9 2.0 convolution_bitcast_fusion
  221.9 2.5 copy.126
  224.4 30.0 %reduce-scatter.6.cloned.1.call-done = f32[32,32,512]{2,1,0:T(8,128)} async-done(((f32[64,32,512]{2,1,0:T(8,128)}), f32[32,32,512]{2,1,0:T(8,128)}) %reduce-scatter.6.cloned.1.call-update) | async-done | bytes 2097168 | tf_op jit(solution)/shard_map/reduce_scatter | solution.py:72
  254.7 2.3 fusion.36
  257.2 2.9 fusion.91
  260.0 4.5 fusion.42
  264.5 5.2 fusion.39
  269.7 2.1 fusion.47
  271.9 6.6 fusion.145
  279.7 1.4 dynamic-update-slice.5
  281.1 123.3 %reduce-scatter.8.cloned.1.call-done = f32[1,32,512]{2,1,0:T(8,128)} async-done(((f32[32,32,512]{2,1,0:T(8,128)}), f32[1,32,512]{2,1,0:T(8,128)}) %reduce-scatter.8.cloned.1.call-update) | async-done | bytes 65552 | tf_op jit(solution)/shard_map/reduce_scatter | solution.py:73
  404.4 1.5 multiply_reduce_fusion.12
  406.0 277.5 %reduce-scatter.4.cloned.1.call-done = f32[32,1536]{1,0:T(8,128)} async-done(((f32[2048,1536]{1,0:T(8,128)}), f32[32,1536]{1,0:T(8,128)}) %reduce-scatter.4.cloned.1.call-update) | async-done | bytes 196624 | tf_op jit(solution)/shard_map/reduce_scatter | solution.py:263
  683.5 1.6 multiply_reduce_fusion.11
  687.7 47.7 %all-reduce.11 = (f32[4]{0:T(128)S(1)}, f32[4]{0:T(128)S(1)}) all-reduce(f32[4]{0:T(128)S(1)} %dynamic-update-slice, f32[4]{0:T(128)S(1)} %dynamic-update-slice.5), channel_id=1, replica_groups=mesh['dp_0'=4,'dp_1'=4,'dp_2'=2,'dp_3'=2,'mp'=2] {'dp_0'}, use_global_device_ids=true, to_apply=%add | all-reduce | flops 8 | bytes 64
  736.7 1.4 dynamic-update-slice.6
  738.1 1.4 dynamic-update-slice.1
  740.0 18.3 %all-reduce.10 = (f32[4]{0:T(128)S(1)}, f32[4]{0:T(128)S(1)}) all-reduce(f32[4]{0:T(128)S(1)} %dynamic-update-slice.1, f32[4]{0:T(128)S(1)} %dynamic-update-slice.6), channel_id=1, replica_groups=mesh['dp_0'=4,'dp_1'=4,'dp_2'=2,'dp_3'=2,'mp'=2] {'dp_1'}, use_global_device_ids=true, to_apply=%add.1 | all-reduce | flops 8 | bytes 64
  759.6 1.4 dynamic-update-slice.7
  761.0 1.4 dynamic-update-slice.2
  763.0 4.9 all-reduce.14
  769.1 1.4 dynamic-update-slice.8
  770.5 1.4 dynamic-update-slice.3
  772.5 2.4 all-reduce.13
  776.1 1.4 dynamic-update-slice.9
  777.5 1.4 dynamic-update-slice.4
  778.9 6.4 all-reduce.12
  (184 shorter events, 36.6 us)
Async XLA Ops:
  7.2 33.6 %copy-start = (bf16[2048,512]{1,0:T(8,128)(2,1)S(1)}, bf16[2048,512]{1,0:T(8,128)(2,1)}, u32[]{:S(2)}) copy-start(bf16[2048,512]{1,0:T(8,128)(2,1)} %param.28) | copy-start | bytes 6291460
  7.2 135.0 %all-gather.2.cloned.1.call-start = ((), (), s32[]{:S(2)}) async-start(), calls=%async_computation.8 | async-start | bytes 8519680 | tf_op jit(solution)/shard_map/all_gather | solution.py:41
  22.2 3.7 copy-start.13
  25.9 2.0 copy-start.4
  25.9 2.4 copy-start.8
  25.9 4.0 copy-start.7
  27.9 1.4 copy-start.5
  42.9 6.0 copy-start.22
  42.9 32.9 %all-to-all-start.1 = ((f32[2,128,2048]{2,1,0:T(8,128)}), f32[2,128,2048]{2,1,0:T(8,128)}, u32[]{:S(2)}, u32[]{:S(2)}) async-start(f32[2,128,2048]{2,1,0:T(8,128)} %fusion.11), calls=%async_computation.1 | async-start | bytes 4194304 | tf_op jit(solution)/shard_map/all_to_all | solution.py:32
  52.1 1.3 copy-start.2
  52.1 1.7 copy-start.19
  52.1 1.9 copy-start.9
  52.1 90.1 %copy-start.30 = (f32[256]{0:T(256)}, f32[256]{0:T(256)S(1)}, u32[]{:S(2)}) copy-start(f32[256]{0:T(256)S(1)} %broadcast_multiply_fusion.3) | copy-start | bytes 3076
  53.8 88.4 %copy-start.32 = (f32[256]{0:T(256)}, f32[256]{0:T(256)S(1)}, u32[]{:S(2)}) copy-start(f32[256]{0:T(256)S(1)} %add_rsqrt_fusion.2) | copy-start | bytes 3076
  55.0 25.7 %copy-start.23 = (f32[128,16]{0,1:T(8,128)}, f32[128,16]{0,1:T(8,128)S(1)}, u32[]{:S(2)}) copy-start(f32[128,16]{0,1:T(8,128)S(1)} %copy.148) | copy-start | bytes 24580
  78.6 2.1 copy-start.16
  78.6 9.5 %copy-start.34 = (f32[8]{0:T(128)S(1)}, f32[8]{0:T(128)}, u32[]{:S(2)}) copy-start(f32[8]{0:T(128)} %param.23) | copy-start | bytes 100
  78.6 14.9 %copy-start.14 = (f32[16,2048]{1,0:T(8,128)S(1)}, f32[16,2048]{1,0:T(8,128)}, u32[]{:S(2)}) copy-start(f32[16,2048]{1,0:T(8,128)} %param.24) | copy-start | bytes 393220
  84.9 8.6 %all-to-all-start.2 = ((f32[2,128,16]{1,2,0:T(8,128)}), f32[2,128,16]{1,2,0:T(8,128)S(1)}, u32[]{:S(2)}, u32[]{:S(2)}) async-start(f32[2,128,16]{1,2,0:T(8,128)} %broadcast_in_dim.4), calls=%async_computation.2 | async-start | bytes 32768 | tf_op jit(solution)/shard_map/all_to_all | solution.py:54
  96.7 1.4 copy-start.6
  104.1 1.9 copy-start.12
  109.2 31.1 %all-to-all-start.3 = ((f32[2,128,2048]{2,1,0:T(8,128)}), f32[2,128,2048]{2,1,0:T(8,128)}, u32[]{:S(2)}, u32[]{:S(2)}) async-start(f32[2,128,2048]{2,1,0:T(8,128)} %fusion.9), calls=%async_computation.3 | async-start | bytes 4194304 | tf_op jit(solution)/shard_map/all_to_all | solution.py:32
  114.3 27.9 %copy-start.3 = (f32[256,2048]{1,0:T(8,128)S(1)}, f32[256,2048]{1,0:T(8,128)}, u32[]{:S(2)}) copy-start(f32[256,2048]{1,0:T(8,128)} %copy-done.2) | copy-start | bytes 6291460
  153.4 2.7 copy-start.40
  160.9 5.0 copy-start.29
  160.9 30.1 %all-to-all-start = ((f32[2,128,2048]{2,1,0:T(8,128)}), f32[2,128,2048]{2,1,0:T(8,128)}, u32[]{:S(2)}, u32[]{:S(2)}) async-start(f32[2,128,2048]{2,1,0:T(8,128)} %fusion.13), calls=%async_computation | async-start | bytes 4194304 | tf_op jit(solution)/shard_map/all_to_all | solution.py:32
  165.8 88.6 %reduce-scatter.6.cloned.1.call-start = ((), (), s32[]{:S(2)}) async-start(), calls=%async_computation.10 | async-start | bytes 6291456 | tf_op jit(solution)/shard_map/reduce_scatter | solution.py:72
  167.6 25.2 %copy-start.25 = (f32[1,1,2048]{2,0,1:T(1,128)S(1)}, f32[1,1,2048]{2,0,1:T(1,128)}, u32[]{:S(2)}) copy-start(f32[1,1,2048]{2,0,1:T(1,128)} %get-tuple-element.56) | copy-start | bytes 24580
  192.8 0.9 copy-start.15
  192.8 0.9 copy-start.24
  192.9 0.9 copy-start.28
  217.0 2.9 copy-start.11
  224.4 180.1 %reduce-scatter.8.cloned.1.call-start = ((), (), s32[]{:S(2)}) async-start(), calls=%async_computation.11 | async-start | bytes 2162688 | tf_op jit(solution)/shard_map/reduce_scatter | solution.py:73
  254.4 429.1 %reduce-scatter.4.cloned.1.call-start = ((), (), s32[]{:S(2)}) async-start(), calls=%async_computation.9 | async-start | bytes 12779520 | tf_op jit(solution)/shard_map/reduce_scatter | solution.py:263
  257.0 3.0 copy-start.10
  257.0 3.0 copy-start.41
  269.7 2.1 copy-start.18
  269.7 2.2 copy-start.31
  269.7 2.2 copy-start.33
  278.5 0.7 copy-start.39
  278.5 408.7 %copy-start.38 = (u32[128]{0:T(128)S(1)}, u32[128]{0:T(128)}, u32[]{:S(2)}) copy-start(u32[128]{0:T(128)} %constant.109) | copy-start | bytes 1540
  278.5 461.0 %copy-start.37 = (u32[128]{0:T(128)S(1)}, u32[128]{0:T(128)}, u32[]{:S(2)}) copy-start(u32[128]{0:T(128)} %constant.114) | copy-start | bytes 1540
  278.5 483.9 %copy-start.36 = (u32[128]{0:T(128)S(1)}, u32[128]{0:T(128)}, u32[]{:S(2)}) copy-start(u32[128]{0:T(128)} %constant.119) | copy-start | bytes 1540
  278.5 493.4 %copy-start.35 = (u32[128]{0:T(128)S(1)}, u32[128]{0:T(128)}, u32[]{:S(2)}) copy-start(u32[128]{0:T(128)} %constant.124) | copy-start | bytes 1540
  278.5 509.3 %copy-start.20 = (f32[32,3,512]{2,0,1:T(8,128)S(1)}, f32[32,3,512]{2,0,1:T(8,128)}, u32[]{:S(2)}) copy-start(f32[32,3,512]{2,0,1:T(8,128)} %param.35) | copy-start | bytes 589828
  278.5 509.3 %copy-start.21 = (f32[32,3,512]{2,0,1:T(8,128)S(1)}, f32[32,3,512]{2,0,1:T(8,128)}, u32[]{:S(2)}) copy-start(f32[32,3,512]{2,0,1:T(8,128)} %param.34) | copy-start | bytes 589828
  278.6 513.2 %copy-start.26 = (f32[32,512]{1,0:T(8,128)S(1)}, f32[32,512]{1,0:T(8,128)}, u32[]{:S(2)}) copy-start(f32[32,512]{1,0:T(8,128)} %param.37) | copy-start | bytes 196612
  278.6 513.2 %copy-start.27 = (f32[32,512]{1,0:T(8,128)S(1)}, f32[32,512]{1,0:T(8,128)}, u32[]{:S(2)}) copy-start(f32[32,512]{1,0:T(8,128)} %param.36) | copy-start | bytes 196612
  404.4 387.4 %copy-start.17 = (f32[1,32,512]{2,1,0:T(8,128)S(1)}, f32[1,32,512]{2,1,0:T(8,128)}, u32[]{:S(2)}) copy-start(f32[1,32,512]{2,1,0:T(8,128)} %reduce-scatter.8.cloned.1.call-done) | copy-start | bytes 196612
  687.7 104.7 %copy-start.1 = (bf16[2048,512]{1,0:T(8,128)(2,1)S(1)}, bf16[2048,512]{1,0:T(8,128)(2,1)}, u32[]{:S(2)}) copy-start(bf16[2048,512]{1,0:T(8,128)(2,1)} %param.28) | copy-start | bytes 6291460
Sparse Core Ops, SparseCore 0:
  10.3 113.5 all-gather.1
  224.5 29.8 reduce-scatter.5
  256.8 147.5 reduce-scatter.7
  406.7 276.7 reduce-scatter.3
